TPU v7x, 32 devices: a whole 2x2x4 slice. The times are simulated.
32 devices in a mesh: sub: 2 (over x), vox: 16 (over z, y, core).
Axes of the slice: x: 2, y: 2, z: 4, core: 2. Of those that a mesh axis runs over, the one named last changes fastest.
Arguments:
- observed: float32 [2048, 32768], P('sub', 'vox'), may hold values from -6 to 6
- covariates: float32 [2048, 64], P('sub'), may hold values from -0.26516504 to 0.26516504
- voxel_mask: int32 [32768], P('vox'), may hold values 0 or 1
- tau_index: int32 [1], replicated, may hold values from 2 to 18
Outputs:
- coefficients: float32 [64, 32768], P(None, 'vox')
- split_residual: float32 [2048, 32768], P('sub', 'vox')
All inputs are finite; a program needn't handle non-finite values. Where the computation divides by a largest or mean magnitude, that divisor is 1e-20 or more. No bound on the sum of `voxel_mask` on one device may be relied on, other than what follows from the above.
Results may differ from a plain program's by a relative error of at most 0.0001.
Values sent between devices are 32-bit elements; how exact they have to be, the bound alone decides.
No kernel may reach another device: no remote copies, remote signals or barrier semaphores. Data moves between devices by JAX's collectives and lax.ppermute only.
A program may use at most 128 MiB of HBM per device.

v0:
```python
import functools

import jax
import jax.numpy as jnp
from jax import lax
from jax.experimental import pallas as pl
from jax.experimental.pallas import tpu as pltpu
from jax.sharding import PartitionSpec as P


COVARS = 64
PX = 8
PY = 8
GZ = 32
NPY = 8
QUANT = 20
LANES = 128

LAYER = PY * GZ
HALVES = LAYER // LANES
PER_TILE = LANES // GZ
CHUNKS = ((PX - 1, 0), (1, 2), (3, 4), (5, 6))
EARLY = 2
GROUP = 8
FINISH = ((0, 1), (2, 3))
ROWS = 256
LIMIT = 16 << 20

penalty_fit = 1.0
penalty_tv = 1.0
tv_weight = 0.05
huber_width = 0.02
CLIP_TV = tv_weight / penalty_tv
KAPPA = CLIP_TV / (huber_width + CLIP_TV)

F32 = jnp.float32
BF16 = jnp.bfloat16

VMEM = pl.BlockSpec(memory_space=pltpu.VMEM)
SMEM = pl.BlockSpec(memory_space=pltpu.SMEM)
ANY = pl.BlockSpec(memory_space=pl.ANY)
HBM = pl.BlockSpec(memory_space=pltpu.HBM)


def moved(block, axis, distance):
    size = lax.axis_size(axis)
    route = [((i - distance) % size, i) for i in range(size)]
    return lax.ppermute(block, axis, route)


def others_sum(block, axis):
    received = moved(block, axis, 1)
    for distance in range(2, lax.axis_size(axis)):
        received = received + moved(block, axis, distance)
    return received


def windows(layers):
    runs = []
    for place, layer in enumerate(layers):
        if runs and runs[-1][0] + runs[-1][2] == layer * LAYER:
            runs[-1][2] += LAYER
        else:
            runs.append([layer * LAYER, place * LAYER, LAYER])
    return runs


def dot(a, b):
    return jnp.dot(a, b, preferred_element_type=F32)


def halves(value):
    high = value.astype(BF16)
    return high, (value - high.astype(F32)).astype(BF16)


def columns_of(ref, layers, rows=slice(None)):
    return jnp.concatenate([ref[rows, first : first + width] for first, _, width in windows(layers)], 1)


def copies(source, target, sems, layers, into_chunk):
    plan = []
    for block in range(source.shape[0] // ROWS):
        rows = pl.ds(block * ROWS, ROWS)
        row = []
        for number, (first, place, width) in enumerate(windows(layers)):
            far, near = (rows, pl.ds(first, width)), (rows, pl.ds(place, width))
            src, dst = (far, near) if into_chunk else (near, far)
            row.append(pltpu.make_async_copy(source.at[src], target.at[dst], sems.at[block, number]))
        plan.append(row)
    return plan


def start(row):
    for copy in row:
        copy.start()


def wait(row):
    for copy in row:
        copy.wait()


def call(kernel, out_shape, in_specs, out_specs, scratch, flops, args, aliases=None):
    return pl.pallas_call(
        kernel,
        out_shape=out_shape,
        in_specs=in_specs,
        out_specs=out_specs,
        scratch_shapes=scratch,
        input_output_aliases=aliases or {},
        cost_estimate=pl.CostEstimate(flops=flops, bytes_accessed=4 << 20, transcendentals=0),
        compiler_params=pltpu.CompilerParams(vmem_limit_bytes=LIMIT),
    )(*args)


def sds(*shape, dtype=F32):
    return jax.ShapeDtypeStruct(shape, dtype)


def prepare_kernel(tau, place, cov, xt, xe, gram, setup):
    row = lax.broadcasted_iota(jnp.int32, setup.shape, 0)
    quantile = jnp.full(setup.shape, tau[0], jnp.int32).astype(F32) / QUANT
    pencil_y = jnp.full(setup.shape, place[0], jnp.int32)
    keep_prev = jnp.where(pencil_y > 0, 1.0, 0.0)
    keep_next = jnp.where(pencil_y < NPY - 1, 1.0, 0.0)
    setup[...] = jnp.where(row == 0, quantile, jnp.where(row == 1, keep_prev, keep_next))
    high, low = halves(cov[...])
    both = jnp.concatenate([high, low], 0)
    xt[...] = both
    turned = both.astype(F32).T.astype(BF16)
    xe[...] = jnp.concatenate([turned, turned], 1)
    summed = dot(both, turned)
    summed = summed[:COVARS] + summed[COVARS:]
    gram[...] = summed + pltpu.roll(summed, COVARS, 1)


def prepare(tau, place, cov):
    rows = cov.shape[1]
    out = (sds(2 * COVARS, rows, dtype=BF16), sds(rows, 4 * COVARS, dtype=BF16), sds(COVARS, LANES), sds(8, LANES))
    return call(prepare_kernel, out, [SMEM, SMEM, VMEM], (VMEM,) * 4, [], 1 << 24, (tau, place, cov))


def first_kernel(layers, opening, *refs):
    obs, xt, *gram, part = refs
    width = len(layers) * LAYER
    if opening:
        part[:, width:] = gram[0][...]
    total = None
    for block in range(obs.shape[0] // ROWS):
        rows = slice(block * ROWS, (block + 1) * ROWS)
        high, low = halves(columns_of(obs, layers, rows))
        term = dot(xt[:, rows], high) + dot(xt[:, rows], low)
        total = term if total is None else total + term
    part[:, :width] = total[:COVARS] + total[COVARS:]


def first_stage(layers, args, opening):
    rows, width = args[0].shape[0], len(layers) * LAYER
    out = sds(COVARS, width + (LANES if opening else 0))
    flops = 2 * rows * 2 * COVARS * 2 * width
    kernel = functools.partial(first_kernel, layers, opening)
    return call(kernel, out, [VMEM] * len(args), VMEM, [], flops, args)


def packed_rows(chunks, lane):
    at = lax.broadcasted_iota(jnp.int32, (COVARS, LANES), 1) // GZ
    tiles = []
    for tile in range(PX // PER_TILE):
        built = None
        for place in range(PER_TILE):
            layer = tile * PER_TILE + place
            number = next(n for n, layers in enumerate(CHUNKS) if layer in layers)
            first = CHUNKS[number].index(layer) * LAYER + lane * GZ
            base = first // LANES * LANES
            piece = chunks[number][:, base : base + LANES]
            shift = (place * GZ - (first - base)) % LANES
            piece = pltpu.roll(piece, shift, 1) if shift else piece
            built = piece if built is None else jnp.where(at == place, piece, built)
        tiles.append(built)
    return jnp.concatenate(tiles, 1)


def updated(stage, eta, mask, layers, own, got, base, grad):
    width = len(layers) * LAYER
    scale = eta * columns_of(mask, layers).astype(F32)
    summed = penalty_fit * (own[:, :width] + got[:, :width])
    if stage == 1:
        return scale * summed, None
    now = base[...] + (2.0 * scale) * summed - (eta * penalty_tv) * grad[...]
    return now, now - scale * summed


def coef_kernel(stage, *refs):
    refs = list(refs)
    take = lambda: refs.pop(0)
    mask, eta = take(), take()[0:1, 0:1]
    sums = [[take() for _ in range(2 if stage == 1 else 4)] for _ in CHUNKS[EARLY:]]
    order = [take() for _ in range(EARLY)]
    for layers, (own, got, *old) in zip(CHUNKS[EARLY:], sums):
        coef = take()
        order.append(coef)
        now, rest = updated(stage, eta, mask, layers, own, got, *(old or (None, None)))
        coef[...] = now
        if stage == 2:
            take()[...] = rest
    heads, tails = refs
    heads[...] = packed_rows(order, 0)
    tails[...] = packed_rows(order, PY - 1)


def coef_stage(stage, mask, eta, sums, earlier):
    args = [mask, eta] + [a for group in sums for a in group] + list(earlier)
    out = []
    for layers in CHUNKS[EARLY:]:
        out += [sds(COVARS, len(layers) * LAYER)] * stage
    out += [sds(COVARS, PX * GZ)] * 2
    kernel = functools.partial(coef_kernel, stage)
    results = list(call(kernel, tuple(out), [VMEM] * len(args), (VMEM,) * len(out), [], 1 << 20, args))
    return results[:-2:stage], results[1:-2:2] if stage == 2 else [], *results[-2:]


def step_kernel(layers, stage, opening, update, *refs):
    refs = list(refs)
    take = lambda: refs.pop(0)
    setup = take()
    if update:
        mask, own, got = take(), take(), take()
        eta = None if opening else take()[0:1, 0:1]
        base, grad = (take(), take()) if stage > 1 else (None, None)
    else:
        given = take()
    xe, xt, y = [take() for _ in range(3)]
    state = take() if stage > 1 else None
    if update:
        coef = take()
        eta_out = take() if opening else None
        carry = take() if stage > 1 else None
        sides = take() if PX - 1 in layers else None
    part, state_out, bext = [take() for _ in range(3)]

    width = len(layers) * LAYER
    if update:
        if opening:
            gram = jnp.abs(own[:, width:] + got[:, width:])
            first_half = lax.broadcasted_iota(jnp.int32, gram.shape, 1) < COVARS
            bound = jnp.max(jnp.sum(jnp.where(first_half, gram, 0.0), 0, keepdims=True), 1, keepdims=True)
            eta = 1.0 / (penalty_fit * bound + 12.0 * penalty_tv)
            eta_out[...] = jnp.broadcast_to(eta, eta_out.shape)
        now, rest = updated(stage, eta, mask, layers, own, got, base, grad)
        coef[...] = now
        if stage > 1:
            carry[...] = rest
        if sides is not None:
            for spot, layer in enumerate((PX - 1, 0)):
                first = layers.index(layer) * LAYER
                sides[:, spot * LAYER : (spot + 1) * LAYER] = now[:, first : first + LAYER]
    else:
        now = given[...]
    quantile = jnp.broadcast_to(setup[0:1, 0:1], (1, width))
    lower, upper = (quantile - 1.0) / penalty_fit, quantile / penalty_fit
    high, low = halves(now)
    bext[...] = jnp.concatenate([high, high, low, low], 0)
    total = None
    blocks = y.shape[0] // ROWS
    following = dot(xe[:ROWS, :], bext[...])
    for block in range(blocks):
        rows = slice(block * ROWS, (block + 1) * ROWS)
        fit = following
        if block + 1 < blocks:
            following = dot(xe[(block + 1) * ROWS : (block + 2) * ROWS, :], bext[...])
        image = columns_of(y, layers, rows)
        dual = jnp.clip((image if stage == 1 else state[rows, :]) - fit, lower, upper)
        state_out[rows, :] = image + dual
        high, low = halves(dual)
        term = dot(xt[:, rows], high) + dot(xt[:, rows], low)
        total = term if total is None else total + term
    part[...] = total[:COVARS] + total[COVARS:]


def step_stage(layers, stage, opening, setup, head, heavy):
    width, rows = len(layers) * LAYER, heavy[2].shape[0]
    update = len(head) > 1
    args = [setup] + [a for a in head + heavy if a is not None]
    specs = [VMEM] * len(args)
    out = []
    if update:
        out.append(sds(COVARS, width))
        out += [sds(8, LANES)] if opening else []
        out += [sds(COVARS, width)] if stage > 1 else []
        out += [sds(COVARS, 2 * LAYER)] if PX - 1 in layers else []
    out += [sds(COVARS, width), sds(rows, width)]
    scratch = [pltpu.VMEM((4 * COVARS, width), BF16)]
    kernel = functools.partial(step_kernel, layers, stage, opening, update)
    flops = 2 * rows * width * 2 * (2 * COVARS + 2 * COVARS)
    return list(call(kernel, tuple(out), specs, (VMEM,) * len(out), scratch, flops, args))


def tv_kernel(passes, edge, *refs):
    refs = list(refs)
    fields = []
    for _ in range(passes):
        chunks = [refs.pop(0) for _ in CHUNKS]
        from_left, from_right = refs.pop(0), refs.pop(0)
        heads, tails, before, after = [refs.pop(0) for _ in range(4)]
        fields.append((chunks, from_left, from_right, heads, tails, before, after))
    outs = refs
    place_of = {layer: (n, c.index(layer)) for n, c in enumerate(CHUNKS) for layer in c}
    lane = lax.broadcasted_iota(jnp.int32, (GROUP, LANES), 1)

    def one_group(group, carry):
        rows = pl.ds(pl.multiple_of(group * GROUP, GROUP), GROUP)
        keep_prev, keep_y = edge[1:2, :], edge[2:3, :]

        def tile(field, layer, half):
            chunks, from_left, from_right = field[:3]
            if layer < 0:
                return from_left[rows, half * LANES : (half + 1) * LANES]
            if layer == PX:
                return from_right[rows, LAYER + half * LANES : LAYER + (half + 1) * LANES]
            number, place = place_of[layer]
            first = place * LAYER + half * LANES
            return chunks[number][rows, first : first + LANES]

        def dual_of(steps):
            q = None
            for step in steps[:-1]:
                q = jnp.clip((step if q is None else step + q) * KAPPA, -CLIP_TV, CLIP_TV)
            step = steps[-1] if q is None else steps[-1] + q
            twice = jnp.clip(step * (2.0 * KAPPA), -2.0 * CLIP_TV, 2.0 * CLIP_TV)
            return twice if q is None else twice - q

        def dual_x(layer, half):
            return dual_of([tile(f, layer + 1, half) - tile(f, layer, half) for f in fields])

        def dual_z(layer, half):
            steps = []
            for f in fields:
                now = tile(f, layer, half)
                steps.append(jnp.where(lane % GZ == GZ - 1, 0.0, pltpu.roll(now, LANES - 1, 1) - now))
            return dual_of(steps)

        def dual_y(layer, half):
            steps = []
            group_at, spot = layer // PER_TILE, layer % PER_TILE
            for f in fields:
                now = tile(f, layer, half)
                if half + 1 < HALVES:
                    after = pltpu.roll(tile(f, layer, half + 1), LANES - GZ, 1)
                else:
                    after = f[6][rows, group_at * LANES : (group_at + 1) * LANES]
                    shift = (LANES - GZ - spot * GZ) % LANES
                    after = pltpu.roll(after, shift, 1) if shift else after
                following = jnp.where(lane < LANES - GZ, pltpu.roll(now, LANES - GZ, 1), after)
                step = following - now
                if half + 1 == HALVES:
                    step = step * jnp.where(lane < LANES - GZ, 1.0, keep_y)
                steps.append(step)
            return dual_of(steps)

        edge_duals = []
        for group_at in range(PX // PER_TILE):
            at = slice(group_at * LANES, (group_at + 1) * LANES)
            edge_duals.append(dual_of([(f[3][rows, at] - f[5][rows, at]) * keep_prev for f in fields]))

        before_x = [dual_x(-1, half) for half in range(HALVES)]
        for layer in range(PX):
            number, place = place_of[layer]
            group_at, spot = layer // PER_TILE, layer % PER_TILE
            shift = (LANES - spot * GZ) % LANES
            before_y = pltpu.roll(edge_duals[group_at], shift, 1) if shift else edge_duals[group_at]
            for half in range(HALVES):
                x_now = dual_x(layer, half)
                y_now = dual_y(layer, half)
                z_now = dual_z(layer, half)
                rolled = pltpu.roll(y_now, GZ, 1)
                summed = before_x[half] - x_now
                summed = summed + (jnp.where(lane < GZ, before_y, rolled) - y_now)
                summed = summed + (pltpu.roll(z_now, 1, 1) - z_now)
                first = place * LAYER + half * LANES
                outs[number][rows, first : first + LANES] = summed
                before_x[half] = x_now
                before_y = rolled
        return carry

    lax.fori_loop(0, COVARS // GROUP, one_group, 0)


def tv_stage(edge, fields):
    args, specs = [edge], [VMEM]
    for chunks, *rest in fields:
        args += list(chunks) + rest
        specs += [VMEM] * (len(chunks) + len(rest))
    out = tuple(sds(COVARS, len(c) * LAYER) for c in CHUNKS)

    def kernel(edge_ref, *refs):
        tv_kernel(len(fields), edge_ref, *refs)

    flops = len(fields) * 60 * COVARS * PX * LAYER * 64
    return call(kernel, out, specs, (VMEM,) * len(out), [], flops, args)


def last_kernel(group, first, *refs):
    refs = list(refs)
    take = lambda: refs.pop(0)
    setup, mask, eta, xe = [take() for _ in range(4)]
    chunks = [[take() for _ in range(5)] for _ in group]
    if not first:
        take(), take()
    coef_out, res_out = take(), take()
    step = eta[0:1, 0:1]
    plan = []
    for layers, (own, got, base, grad, state) in zip(group, chunks):
        bext, rbuf, rsems, cbuf, csems = [take() for _ in range(5)]
        width = len(layers) * LAYER
        kept = columns_of(mask, layers).astype(F32)
        quantile = jnp.broadcast_to(setup[0:1, 0:1], (1, width))
        lower, upper = (quantile - 1.0) / penalty_fit, quantile / penalty_fit
        summed = penalty_fit * (own[:, :width] + got[:, :width])
        now = base[...] + (2.0 * step * kept) * summed - (step * penalty_tv) * grad[...]
        cbuf[...] = now
        coef_stores = []
        for number, (at, place, span) in enumerate(windows(layers)):
            coef_stores.append(
                pltpu.make_async_copy(cbuf.at[:, pl.ds(place, span)], coef_out.at[:, pl.ds(at, span)], csems.at[number])
            )
        start(coef_stores)
        high, low = halves(now)
        bext[...] = jnp.concatenate([high, high, low, low], 0)
        stores = copies(rbuf, res_out, rsems, layers, False)
        for block, row in enumerate(stores):
            rows = slice(block * ROWS, (block + 1) * ROWS)
            target = state[rows, :] - dot(xe[rows, :], bext[...])
            rbuf[rows, :] = kept * (target - jnp.clip(target, lower, upper))
            start(row)
        plan += [coef_stores] + stores
    for row in plan:
        wait(row)


def last_stage(group, pencil, setup, mask, eta, xe, chunks, outs):
    rows = xe.shape[0]
    args, specs = [setup, mask, eta, xe], [VMEM] * 4
    for chunk in chunks:
        args, specs = args + list(chunk), specs + [VMEM] * len(chunk)
    aliases = {}
    if outs is not None:
        aliases = {len(args): 0, len(args) + 1: 1}
        args, specs = args + list(outs), specs + [HBM, HBM]
    scratch, flops = [], 0
    for layers in group:
        width, runs = len(layers) * LAYER, len(windows(layers))
        scratch += [
            pltpu.VMEM((4 * COVARS, width), BF16),
            pltpu.VMEM((rows, width), F32),
            pltpu.SemaphoreType.DMA((rows // ROWS, runs)),
            pltpu.VMEM((COVARS, width), F32),
            pltpu.SemaphoreType.DMA((runs,)),
        ]
        flops += 2 * rows * width * 4 * COVARS * 2
    out = (sds(COVARS, pencil), sds(rows, pencil))
    kernel = functools.partial(last_kernel, group, outs is None)
    return call(kernel, out, specs, (HBM, HBM), scratch, flops, args, aliases)


def neighbours_x(chunk):
    size = lax.axis_size("vox")
    before = moved(chunk, "vox", NPY)
    after = before if (2 * NPY) % size == 0 else moved(chunk, "vox", -NPY)
    return before, after


def per_device(observed, covariates, voxel_mask, tau_index):
    pencils = lax.axis_size("vox")
    pencil_y = (lax.axis_index("vox") + NPY // 2) % pencils % NPY
    mask = voxel_mask.reshape(1, -1)

    parts = []
    xt, xe, gram, setup = prepare(tau_index, pencil_y.reshape(1), covariates.T)
    for number, layers in enumerate(CHUNKS):
        args = [observed, xt] + ([] if number else [gram])
        part = first_stage(layers, args, number == 0)
        parts.append((part, others_sum(part, "sub")))

    eta, base, grad, states, fields = None, None, None, [None] * len(CHUNKS), []
    for stage in (1, 2):
        coefs, carries, new_parts, new_states = [], [], [], []
        for number, layers in enumerate(CHUNKS):
            opening = eta is None
            update = [mask, *parts[number], eta, base[number] if base else None, grad[number] if grad else None]
            heavy = [xe, xt, observed, states[number]]
            if number < EARLY:
                results = step_stage(layers, stage, opening, setup, update, heavy)
                coefs.append(results.pop(0))
                if opening:
                    eta = results.pop(0)
                if stage == 2:
                    carries.append(results.pop(0))
                if number == 0:
                    from_left, from_right = neighbours_x(results.pop(0))
            if number == EARLY:
                rest = range(EARLY, len(CHUNKS))
                sums = [parts[n] + ((base[n], grad[n]) if stage == 2 else ()) for n in rest]
                more, more_carries, heads, tails = coef_stage(stage, mask, eta, sums, coefs)
                coefs, carries = coefs + more, carries + more_carries
                before = moved(tails, "vox", 1)
                after = moved(heads, "vox", -1)
            if number >= EARLY:
                results = step_stage(layers, stage, False, setup, [coefs[number]], heavy)
            part, state = results
            new_states.append(state)
            new_parts.append((part, others_sum(part, "sub")))
        fields.append((coefs, from_left, from_right, heads, tails, before, after))
        grad = tv_stage(setup, fields)
        base = coefs if stage == 1 else carries
        parts, states = new_parts, new_states

    outs = None
    for members in FINISH:
        chunks = [(*parts[n], base[n], grad[n], states[n]) for n in members]
        group = tuple(CHUNKS[n] for n in members)
        outs = last_stage(group, observed.shape[1], setup, mask, eta, xe, chunks, outs)
    return tuple(outs)


def solution(mesh):
    return jax.shard_map(
        per_device,
        mesh=mesh,
        in_specs=(P("sub", "vox"), P("sub", None), P("vox"), P()),
        out_specs=(P(None, "vox"), P("sub", "vox")),
        check_vma=False,
    )
```

profile of v0, /device:TPU:0, one launch (start us, length us, event | category | flops | bytes accessed | tf_op | source)
XLA Modules:
  0.0 56.8 jit_solution(6383325475726242177)
XLA Ops:
  1.3 0.0 copy-start.3
  1.3 0.9 %copy-done.3 = f32[1024,64]{0,1:T(8,128)S(1)} copy-done((f32[1024,64]{0,1:T(8,128)S(1)}, f32[1024,64]{0,1:T(8,128)}, u32[]{:S(2)}) %copy-start.3) | copy-done | bytes 262168
  2.3 0.4 shard_map.59
  2.6 0.0 copy-start
  2.7 3.4 %copy-done = f32[1024,2048]{1,0:T(8,128)S(1)} copy-done((f32[1024,2048]{1,0:T(8,128)S(1)}, f32[1024,2048]{1,0:T(8,128)}, u32[]{:S(2)}) %copy-start) | copy-done | bytes 8388632
  6.0 0.0 copy-start.1
  6.0 0.5 shard_map.60.refs_2_
  6.5 3.0 %collective-permute-start = (f32[64,640]{1,0:T(8,128)S(1)}, f32[64,640]{1,0:T(8,128)S(1)}, u32[]{:S(2)}, u32[]{:S(2)}) collective-permute-start(f32[64,640]{1,0:T(8,128)S(1)} %shard_map.60.refs_2_), channel_id=1, source_target_pairs={{16,0},{0,16},{17,1},{1,17},{18,2},{2,18},{19,3},{3,19},{20,4},{4,... | collective-permute-start | bytes 491528 | tf_op jit(solution)/shard_map/ppermute | solution.py:48
  9.5 0.0 copy-done.1
  9.5 0.5 shard_map.64.refs_2_
  10.0 2.9 %collective-permute-start.3 = (f32[64,512]{1,0:T(8,128)S(1)}, f32[64,512]{1,0:T(8,128)S(1)}, u32[]{:S(2)}, u32[]{:S(2)}) collective-permute-start(f32[64,512]{1,0:T(8,128)S(1)} %shard_map.64.refs_2_), channel_id=1, source_target_pairs={{16,0},{0,16},{17,1},{1,17},{18,2},{2,18},{19,3},{3,19},{20,4},{4,... | collective-permute-start | bytes 393224 | tf_op jit(solution)/shard_map/ppermute | solution.py:48
  12.9 0.5 shard_map.62.refs_2_
  13.4 0.0 copy-start.2
  13.4 0.1 collective-permute-start.1
  13.5 0.5 shard_map.63.refs_4_
  13.9 2.1 %collective-permute-start.2 = (f32[64,512]{1,0:T(8,128)S(1)}, f32[64,512]{1,0:T(8,128)S(1)}, u32[]{:S(2)}, u32[]{:S(2)}) collective-permute-start(f32[64,512]{1,0:T(8,128)S(1)} %shard_map.63.refs_4_), channel_id=1, source_target_pairs={{16,0},{0,16},{17,1},{1,17},{18,2},{2,18},{19,3},{3,19},{20,4},{4,... | collective-permute-start | bytes 393224 | tf_op jit(solution)/shard_map/ppermute | solution.py:48
  16.0 0.0 collective-permute-done.refs_3_
  16.0 0.0 copy-done.2
  16.0 1.2 %shard_map.61 = (f32[64,512]{1,0:T(8,128)S(1)}, f32[8,128]{1,0:T(8,128)S(1)}, f32[64,512]{1,0:T(8,128)S(1)}, f32[64,512]{1,0:T(8,128)S(1)}, f32[1024,512]{1,0:T(8,128)S(1)}) custom-call(f32[8,128]{1,0:T(8,128)S(1)} %get-tuple-element.51.refs_0_.edge_ref, s32[1,2048]{1,0:T(1,128)S(1)} %bitcast.3, f32[64,640]{1,0:T(8,128)S(1)} %shard_map.60.refs_2_, ...), custom_call_target="tpu_custom_call" | custom-call | flops 536870912 | bytes 4194304 | tf_op jit(solution)/shard_map/pallas_call | solution.py:105
  17.2 2.7 %collective-permute-start.5 = (f32[64,512]{1,0:T(8,128)S(1)}, f32[64,512]{1,0:T(8,128)S(1)}, u32[]{:S(2)}, u32[]{:S(2)}) collective-permute-start(f32[64,512]{1,0:T(8,128)S(1)} %get-tuple-element.61), channel_id=1, source_target_pairs={{8,0},{9,1},{10,2},{11,3},{12,4},{13,5},{14,6},{15,7},{0,8},{1,9},... | collective-permute-start | bytes 393224 | tf_op jit(solution)/shard_map/ppermute | solution.py:48
  19.8 0.5 collective-permute-start.9
  20.4 0.0 collective-permute-done.3.refs_3_
  20.4 1.1 %shard_map.65 = (f32[64,512]{1,0:T(8,128)S(1)}, f32[64,512]{1,0:T(8,128)S(1)}, f32[1024,512]{1,0:T(8,128)S(1)}) custom-call(f32[8,128]{1,0:T(8,128)S(1)} %get-tuple-element.51.refs_0_.edge_ref, s32[1,2048]{1,0:T(1,128)S(1)} %bitcast.4, f32[64,512]{1,0:T(8,128)S(1)} %shard_map.64.refs_2_, f32[64,512]{1,0:T(8,128)S(1)} %collective-permute-done.3.refs_3_, ...), custom_call_target="tpu_custom_call" | custom-call | flops 536870912 | bytes 4194304 | tf_op jit(solution)/shard_map/pallas_call | solution.py:105
  21.5 0.0 collective-permute-done.1.refs_3_
  21.5 1.4 %collective-permute-done.2.refs_5_ = f32[64,512]{1,0:T(8,128)S(1)} collective-permute-done((f32[64,512]{1,0:T(8,128)S(1)}, f32[64,512]{1,0:T(8,128)S(1)}, u32[]{:S(2)}, u32[]{:S(2)}) %collective-permute-start.2) | collective-permute-done | bytes 131104 | tf_op jit(solution)/shard_map/ppermute | solution.py:48
  22.9 0.2 shard_map.66
  23.1 2.9 %collective-permute-start.7 = (f32[64,256]{1,0:T(8,128)S(1)}, f32[64,256]{1,0:T(8,128)S(1)}, u32[]{:S(2)}, u32[]{:S(2)}) collective-permute-start(f32[64,256]{1,0:T(8,128)S(1)} %get-tuple-element.62.refs_6_), channel_id=1, source_target_pairs={{1,0},{2,1},{3,2},{4,3},{5,4},{6,5},{7,6},{8,7},{9,8},{10,9},{11,1... | collective-permute-start | bytes 196616 | tf_op jit(solution)/shard_map/ppermute | solution.py:48
  26.0 0.0 collective-permute-start.6
  26.0 1.5 %collective-permute-start.10 = (f32[64,512]{1,0:T(8,128)S(1)}, f32[64,512]{1,0:T(8,128)S(1)}, u32[]{:S(2)}, u32[]{:S(2)}) collective-permute-start(f32[64,512]{1,0:T(8,128)S(1)} %get-tuple-element.71.refs_2_), channel_id=1, source_target_pairs={{16,0},{0,16},{17,1},{1,17},{18,2},{2,18},{19,3},{3,19},{20,4},{4,... | collective-permute-start | bytes 393224 | tf_op jit(solution)/shard_map/ppermute | solution.py:48
  27.4 1.0 %shard_map.67 = (f32[64,512]{1,0:T(8,128)S(1)}, f32[1024,512]{1,0:T(8,128)S(1)}) custom-call(f32[8,128]{1,0:T(8,128)S(1)} %get-tuple-element.51.refs_0_.edge_ref, f32[64,512]{1,0:T(8,128)S(1)} %get-tuple-element.58.refs_1_.refs_2_.refs_4_, bf16[1024,256]{1,0:T(8,128)(2,1)S(1)} %get-tuple-element.54.refs_4_.refs_5_.refs_2_.refs_7_.refs_3_, ...), custom_call_target="tpu_custom_call" | custom-call | flops 536870912 | bytes 4194304 | tf_op jit(solution)/shard_map/pallas_call | solution.py:105
  28.5 1.0 %shard_map.69 = (f32[64,512]{1,0:T(8,128)S(1)}, f32[1024,512]{1,0:T(8,128)S(1)}) custom-call(f32[8,128]{1,0:T(8,128)S(1)} %get-tuple-element.51.refs_0_.edge_ref, f32[64,512]{1,0:T(8,128)S(1)} %get-tuple-element.60.refs_3_.refs_1_.refs_8_, bf16[1024,256]{1,0:T(8,128)(2,1)S(1)} %get-tuple-element.54.refs_4_.refs_5_.refs_2_.refs_7_.refs_3_, ...), custom_call_target="tpu_custom_call" | custom-call | flops 536870912 | bytes 4194304 | tf_op jit(solution)/shard_map/pallas_call | solution.py:105
  29.5 0.0 collective-permute-done.7.refs_9_
  29.6 0.6 %collective-permute-start.4 = (f32[64,512]{1,0:T(8,128)S(1)}, f32[64,512]{1,0:T(8,128)S(1)}, u32[]{:S(2)}, u32[]{:S(2)}) collective-permute-start(f32[64,512]{1,0:T(8,128)S(1)} %get-tuple-element.59.refs_2_), channel_id=1, source_target_pairs={{16,0},{0,16},{17,1},{1,17},{18,2},{2,18},{19,3},{3,19},{20,4},{4,... | collective-permute-start | bytes 393224 | tf_op jit(solution)/shard_map/ppermute | solution.py:48
  30.2 2.2 %collective-permute-done.6.refs_8_ = f32[64,256]{1,0:T(8,128)S(1)} collective-permute-done((f32[64,256]{1,0:T(8,128)S(1)}, f32[64,256]{1,0:T(8,128)S(1)}, u32[]{:S(2)}, u32[]{:S(2)}) %collective-permute-start.6) | collective-permute-done | bytes 65568 | tf_op jit(solution)/shard_map/ppermute | solution.py:48
  32.3 1.5 %collective-permute-start.8 = (f32[64,512]{1,0:T(8,128)S(1)}, f32[64,512]{1,0:T(8,128)S(1)}, u32[]{:S(2)}, u32[]{:S(2)}) collective-permute-start(f32[64,512]{1,0:T(8,128)S(1)} %get-tuple-element.65.refs_6_), channel_id=1, source_target_pairs={{16,0},{0,16},{17,1},{1,17},{18,2},{2,18},{19,3},{3,19},{20,4},{4,... | collective-permute-start | bytes 393224 | tf_op jit(solution)/shard_map/ppermute | solution.py:48
  33.8 0.0 collective-permute-done.5.refs_4_.refs_5_
  33.8 1.6 %shard_map.68 = (f32[64,512]{1,0:T(8,128)S(1)}, f32[64,512]{1,0:T(8,128)S(1)}, f32[64,512]{1,0:T(8,128)S(1)}, f32[64,512]{1,0:T(8,128)S(1)}) custom-call(f32[8,128]{1,0:T(8,128)S(1)} %get-tuple-element.51.refs_0_.edge_ref, f32[64,512]{1,0:T(8,128)S(1)} %get-tuple-element.56.refs_6_.refs_0_.refs_5_, f32[64,512]{1,0:T(8,128)S(1)} %get-tuple-element.57.refs_7_.refs_1_.refs_5_, ...), custom_call_target="tpu_custom_call" | custom-call | flops 503316480 | bytes 4194304 | tf_op jit(solution)/shard_map/pallas_call | solution.py:105
  35.5 0.0 collective-permute-done.9.refs_3_
  35.5 1.2 %shard_map.70 = (f32[64,512]{1,0:T(8,128)S(1)}, f32[64,512]{1,0:T(8,128)S(1)}, f32[64,512]{1,0:T(8,128)S(1)}, f32[64,512]{1,0:T(8,128)S(1)}, f32[1024,512]{1,0:T(8,128)S(1)}) custom-call(f32[8,128]{1,0:T(8,128)S(1)} %get-tuple-element.51.refs_0_.edge_ref, s32[1,2048]{1,0:T(1,128)S(1)} %bitcast.6, f32[64,512]{1,0:T(8,128)S(1)} %get-tuple-element.67.refs_2_, ...), custom_call_target="tpu_custom_call" | custom-call | flops 536870912 | bytes 4194304 | tf_op jit(solution)/shard_map/pallas_call | solution.py:105
  36.7 0.1 collective-permute-start.12
  36.8 0.6 %collective-permute-start.16 = (f32[64,512]{1,0:T(8,128)S(1)}, f32[64,512]{1,0:T(8,128)S(1)}, u32[]{:S(2)}, u32[]{:S(2)}) collective-permute-start(f32[64,512]{1,0:T(8,128)S(1)} %get-tuple-element.90.refs_4_), channel_id=1, source_target_pairs={{16,0},{0,16},{17,1},{1,17},{18,2},{2,18},{19,3},{3,19},{20,4},{4,... | collective-permute-start | bytes 393224 | tf_op jit(solution)/shard_map/ppermute | solution.py:48
  37.4 0.0 collective-permute-done.10.refs_3_
  37.4 1.1 %shard_map.71 = (f32[64,512]{1,0:T(8,128)S(1)}, f32[64,512]{1,0:T(8,128)S(1)}, f32[64,512]{1,0:T(8,128)S(1)}, f32[1024,512]{1,0:T(8,128)S(1)}) custom-call(f32[8,128]{1,0:T(8,128)S(1)} %get-tuple-element.51.refs_0_.edge_ref, s32[1,2048]{1,0:T(1,128)S(1)} %bitcast.7, f32[64,512]{1,0:T(8,128)S(1)} %get-tuple-element.71.refs_2_, ...), custom_call_target="tpu_custom_call" | custom-call | flops 536870912 | bytes 4194304 | tf_op jit(solution)/shard_map/pallas_call | solution.py:105
  38.5 1.6 %collective-permute-start.17 = (f32[64,512]{1,0:T(8,128)S(1)}, f32[64,512]{1,0:T(8,128)S(1)}, u32[]{:S(2)}, u32[]{:S(2)}) collective-permute-start(f32[64,512]{1,0:T(8,128)S(1)} %get-tuple-element.94.refs_9_), channel_id=1, source_target_pairs={{16,0},{0,16},{17,1},{1,17},{18,2},{2,18},{19,3},{3,19},{20,4},{4,... | collective-permute-start | bytes 393224 | tf_op jit(solution)/shard_map/ppermute | solution.py:48
  40.1 0.0 collective-permute-done.4.refs_3_
  40.1 0.0 collective-permute-done.8.refs_7_
  40.1 0.2 shard_map.72
  40.3 1.6 %collective-permute-start.14 = (f32[64,256]{1,0:T(8,128)S(1)}, f32[64,256]{1,0:T(8,128)S(1)}, u32[]{:S(2)}, u32[]{:S(2)}) collective-permute-start(f32[64,256]{1,0:T(8,128)S(1)} %get-tuple-element.81.refs_16_), channel_id=1, source_target_pairs={{1,0},{2,1},{3,2},{4,3},{5,4},{6,5},{7,6},{8,7},{9,8},{10,9},{11,1... | collective-permute-start | bytes 196616 | tf_op jit(solution)/shard_map/ppermute | solution.py:48
  41.9 0.0 collective-permute-start.13
  41.9 1.0 %shard_map.75 = (f32[64,512]{1,0:T(8,128)S(1)}, f32[1024,512]{1,0:T(8,128)S(1)}) custom-call(f32[8,128]{1,0:T(8,128)S(1)} %get-tuple-element.51.refs_0_.edge_ref, f32[64,512]{1,0:T(8,128)S(1)} %get-tuple-element.79.refs_13_.refs_1_, bf16[1024,256]{1,0:T(8,128)(2,1)S(1)} %get-tuple-element.54.refs_4_.refs_5_.refs_2_.refs_7_.refs_3_, ...), custom_call_target="tpu_custom_call" | custom-call | flops 536870912 | bytes 4194304 | tf_op jit(solution)/shard_map/pallas_call | solution.py:105
  43.0 1.1 %shard_map.73 = (f32[64,512]{1,0:T(8,128)S(1)}, f32[1024,512]{1,0:T(8,128)S(1)}) custom-call(f32[8,128]{1,0:T(8,128)S(1)} %get-tuple-element.51.refs_0_.edge_ref, f32[64,512]{1,0:T(8,128)S(1)} %get-tuple-element.75.refs_1_.refs_12_, bf16[1024,256]{1,0:T(8,128)(2,1)S(1)} %get-tuple-element.54.refs_4_.refs_5_.refs_2_.refs_7_.refs_3_, ...), custom_call_target="tpu_custom_call" | custom-call | flops 536870912 | bytes 4194304 | tf_op jit(solution)/shard_map/pallas_call | solution.py:105
  44.0 0.0 collective-permute-done.14.refs_19_
  44.0 0.8 %collective-permute-start.15 = (f32[64,512]{1,0:T(8,128)S(1)}, f32[64,512]{1,0:T(8,128)S(1)}, u32[]{:S(2)}, u32[]{:S(2)}) collective-permute-start(f32[64,512]{1,0:T(8,128)S(1)} %get-tuple-element.86.refs_9_), channel_id=1, source_target_pairs={{16,0},{0,16},{17,1},{1,17},{18,2},{2,18},{19,3},{3,19},{20,4},{4,... | collective-permute-start | bytes 393224 | tf_op jit(solution)/shard_map/ppermute | solution.py:48
  44.8 3.5 %collective-permute-done.13.refs_18_ = f32[64,256]{1,0:T(8,128)S(1)} collective-permute-done((f32[64,256]{1,0:T(8,128)S(1)}, f32[64,256]{1,0:T(8,128)S(1)}, u32[]{:S(2)}, u32[]{:S(2)}) %collective-permute-start.13) | collective-permute-done | bytes 65568 | tf_op jit(solution)/shard_map/ppermute | solution.py:48
  48.3 0.7 %collective-permute-start.11 = (f32[64,512]{1,0:T(8,128)S(1)}, f32[64,512]{1,0:T(8,128)S(1)}, u32[]{:S(2)}, u32[]{:S(2)}) collective-permute-start(f32[64,512]{1,0:T(8,128)S(1)} %get-tuple-element.77.refs_4_), channel_id=1, source_target_pairs={{16,0},{0,16},{17,1},{1,17},{18,2},{2,18},{19,3},{3,19},{20,4},{4,... | collective-permute-start | bytes 393224 | tf_op jit(solution)/shard_map/ppermute | solution.py:48
  49.0 0.0 collective-permute-done.12.refs_14_.refs_15_
  49.0 2.4 %shard_map.74 = (f32[64,512]{1,0:T(8,128)S(1)}, f32[64,512]{1,0:T(8,128)S(1)}, f32[64,512]{1,0:T(8,128)S(1)}, f32[64,512]{1,0:T(8,128)S(1)}) custom-call(f32[8,128]{1,0:T(8,128)S(1)} %get-tuple-element.51.refs_0_.edge_ref, f32[64,512]{1,0:T(8,128)S(1)} %get-tuple-element.56.refs_6_.refs_0_.refs_5_, f32[64,512]{1,0:T(8,128)S(1)} %get-tuple-element.57.refs_7_.refs_1_.refs_5_, ...), custom_call_target="tpu_custom_call" | custom-call | flops 1006632960 | bytes 4194304 | tf_op jit(solution)/shard_map/pallas_call | solution.py:105
  51.4 0.0 collective-permute-done.16.refs_5_
  51.4 0.0 collective-permute-done.17.refs_10_
  51.4 2.6 %shard_map.76 = (f32[64,2048]{1,0:T(8,128)}, f32[1024,2048]{1,0:T(8,128)}) custom-call(f32[8,128]{1,0:T(8,128)S(1)} %get-tuple-element.51.refs_0_.edge_ref, s32[1,2048]{1,0:T(1,128)S(1)} %bitcast.9, f32[8,128]{1,0:T(8,128)S(1)} %get-tuple-element.55.refs_4_.refs_1_.refs_2_, bf16[1024,256]{1,0:T(8,128)(2,1)S(1)} %get-tuple-element.54.refs_4_.refs_5_.refs_2_.refs_7_.refs_3_, ...), custom_call_target="tpu_custom_call" | custom-call | flops 1073741824 | bytes 4194304 | tf_op jit(solution)/shard_map/pallas_call | solution.py:105
  54.0 0.0 collective-permute-done.15.refs_10_
  54.0 0.0 collective-permute-done.11.refs_5_
  54.1 2.6 %shard_map.77 = (f32[64,2048]{1,0:T(8,128)}, f32[1024,2048]{1,0:T(8,128)}) custom-call(f32[8,128]{1,0:T(8,128)S(1)} %get-tuple-element.51.refs_0_.edge_ref, s32[1,2048]{1,0:T(1,128)S(1)} %bitcast.10, f32[8,128]{1,0:T(8,128)S(1)} %get-tuple-element.55.refs_4_.refs_1_.refs_2_, ...), custom_call_target="tpu_custom_call", output_to_operand_aliasing={{0}: (14, {}), {1}: (15, {})} | custom-call | flops 1073741824 | bytes 4194304 | tf_op jit(solution)/shard_map/pallas_call | solution.py:105
Async XLA Ops:
  1.3 1.0 %copy-start.3 = (f32[1024,64]{0,1:T(8,128)S(1)}, f32[1024,64]{0,1:T(8,128)}, u32[]{:S(2)}) copy-start(f32[1024,64]{0,1:T(8,128)} %param.5) | copy-start | bytes 786436
  2.6 3.4 %copy-start = (f32[1024,2048]{1,0:T(8,128)S(1)}, f32[1024,2048]{1,0:T(8,128)}, u32[]{:S(2)}) copy-start(f32[1024,2048]{1,0:T(8,128)} %refs_4_.7) | copy-start | bytes 25165828
  6.0 3.5 %copy-start.1 = (f32[1024,2048]{1,0:T(8,128)S(1)}, f32[1024,2048]{1,0:T(8,128)}, u32[]{:S(2)}) copy-start(f32[1024,2048]{1,0:T(8,128)} %refs_4_.7) | copy-start | bytes 25165828
  6.5 9.5 %collective-permute-start = (f32[64,640]{1,0:T(8,128)S(1)}, f32[64,640]{1,0:T(8,128)S(1)}, u32[]{:S(2)}, u32[]{:S(2)}) collective-permute-start(f32[64,640]{1,0:T(8,128)S(1)} %shard_map.60.refs_2_), channel_id=1, source_target_pairs={{16,0},{0,16},{17,1},{1,17},{18,2},{2,18},{19,3},{3,19},{20,4},{4,... | collective-permute-start | bytes 491528 | tf_op jit(solution)/shard_map/ppermute | solution.py:48
  10.0 10.4 %collective-permute-start.3 = (f32[64,512]{1,0:T(8,128)S(1)}, f32[64,512]{1,0:T(8,128)S(1)}, u32[]{:S(2)}, u32[]{:S(2)}) collective-permute-start(f32[64,512]{1,0:T(8,128)S(1)} %shard_map.64.refs_2_), channel_id=1, source_target_pairs={{16,0},{0,16},{17,1},{1,17},{18,2},{2,18},{19,3},{3,19},{20,4},{4,... | collective-permute-start | bytes 393224 | tf_op jit(solution)/shard_map/ppermute | solution.py:48
  13.4 2.6 %copy-start.2 = (s32[2048]{0:T(1024)S(1)}, s32[2048]{0:T(1024)}, u32[]{:S(2)}) copy-start(s32[2048]{0:T(1024)} %param.6) | copy-start | bytes 24580
  13.4 8.1 %collective-permute-start.1 = (f32[64,512]{1,0:T(8,128)S(1)}, f32[64,512]{1,0:T(8,128)S(1)}, u32[]{:S(2)}, u32[]{:S(2)}) collective-permute-start(f32[64,512]{1,0:T(8,128)S(1)} %shard_map.62.refs_2_), channel_id=1, source_target_pairs={{16,0},{0,16},{17,1},{1,17},{18,2},{2,18},{19,3},{3,19},{20,4},{4,... | collective-permute-start | bytes 393224 | tf_op jit(solution)/shard_map/ppermute | solution.py:48
  13.9 8.9 %collective-permute-start.2 = (f32[64,512]{1,0:T(8,128)S(1)}, f32[64,512]{1,0:T(8,128)S(1)}, u32[]{:S(2)}, u32[]{:S(2)}) collective-permute-start(f32[64,512]{1,0:T(8,128)S(1)} %shard_map.63.refs_4_), channel_id=1, source_target_pairs={{16,0},{0,16},{17,1},{1,17},{18,2},{2,18},{19,3},{3,19},{20,4},{4,... | collective-permute-start | bytes 393224 | tf_op jit(solution)/shard_map/ppermute | solution.py:48
  17.2 16.7 %collective-permute-start.5 = (f32[64,512]{1,0:T(8,128)S(1)}, f32[64,512]{1,0:T(8,128)S(1)}, u32[]{:S(2)}, u32[]{:S(2)}) collective-permute-start(f32[64,512]{1,0:T(8,128)S(1)} %get-tuple-element.61), channel_id=1, source_target_pairs={{8,0},{9,1},{10,2},{11,3},{12,4},{13,5},{14,6},{15,7},{0,8},{1,9},... | collective-permute-start | bytes 393224 | tf_op jit(solution)/shard_map/ppermute | solution.py:48
  19.8 15.6 %collective-permute-start.9 = (f32[64,512]{1,0:T(8,128)S(1)}, f32[64,512]{1,0:T(8,128)S(1)}, u32[]{:S(2)}, u32[]{:S(2)}) collective-permute-start(f32[64,512]{1,0:T(8,128)S(1)} %get-tuple-element.67.refs_2_), channel_id=1, source_target_pairs={{16,0},{0,16},{17,1},{1,17},{18,2},{2,18},{19,3},{3,19},{20,4},{4,... | collective-permute-start | bytes 393224 | tf_op jit(solution)/shard_map/ppermute | solution.py:48
  23.1 6.5 %collective-permute-start.7 = (f32[64,256]{1,0:T(8,128)S(1)}, f32[64,256]{1,0:T(8,128)S(1)}, u32[]{:S(2)}, u32[]{:S(2)}) collective-permute-start(f32[64,256]{1,0:T(8,128)S(1)} %get-tuple-element.62.refs_6_), channel_id=1, source_target_pairs={{1,0},{2,1},{3,2},{4,3},{5,4},{6,5},{7,6},{8,7},{9,8},{10,9},{11,1... | collective-permute-start | bytes 196616 | tf_op jit(solution)/shard_map/ppermute | solution.py:48
  26.0 6.4 %collective-permute-start.6 = (f32[64,256]{1,0:T(8,128)S(1)}, f32[64,256]{1,0:T(8,128)S(1)}, u32[]{:S(2)}, u32[]{:S(2)}) collective-permute-start(f32[64,256]{1,0:T(8,128)S(1)} %get-tuple-element.63.refs_7_), channel_id=1, source_target_pairs={{15,0},{0,1},{1,2},{2,3},{3,4},{4,5},{5,6},{6,7},{7,8},{8,9},{9,10... | collective-permute-start | bytes 196616 | tf_op jit(solution)/shard_map/ppermute | solution.py:48
  26.0 11.4 %collective-permute-start.10 = (f32[64,512]{1,0:T(8,128)S(1)}, f32[64,512]{1,0:T(8,128)S(1)}, u32[]{:S(2)}, u32[]{:S(2)}) collective-permute-start(f32[64,512]{1,0:T(8,128)S(1)} %get-tuple-element.71.refs_2_), channel_id=1, source_target_pairs={{16,0},{0,16},{17,1},{1,17},{18,2},{2,18},{19,3},{3,19},{20,4},{4,... | collective-permute-start | bytes 393224 | tf_op jit(solution)/shard_map/ppermute | solution.py:48
  29.6 10.5 %collective-permute-start.4 = (f32[64,512]{1,0:T(8,128)S(1)}, f32[64,512]{1,0:T(8,128)S(1)}, u32[]{:S(2)}, u32[]{:S(2)}) collective-permute-start(f32[64,512]{1,0:T(8,128)S(1)} %get-tuple-element.59.refs_2_), channel_id=1, source_target_pairs={{16,0},{0,16},{17,1},{1,17},{18,2},{2,18},{19,3},{3,19},{20,4},{4,... | collective-permute-start | bytes 393224 | tf_op jit(solution)/shard_map/ppermute | solution.py:48
  32.3 7.7 %collective-permute-start.8 = (f32[64,512]{1,0:T(8,128)S(1)}, f32[64,512]{1,0:T(8,128)S(1)}, u32[]{:S(2)}, u32[]{:S(2)}) collective-permute-start(f32[64,512]{1,0:T(8,128)S(1)} %get-tuple-element.65.refs_6_), channel_id=1, source_target_pairs={{16,0},{0,16},{17,1},{1,17},{18,2},{2,18},{19,3},{3,19},{20,4},{4,... | collective-permute-start | bytes 393224 | tf_op jit(solution)/shard_map/ppermute | solution.py:48
  36.7 12.3 %collective-permute-start.12 = (f32[64,512]{1,0:T(8,128)S(1)}, f32[64,512]{1,0:T(8,128)S(1)}, u32[]{:S(2)}, u32[]{:S(2)}) collective-permute-start(f32[64,512]{1,0:T(8,128)S(1)} %get-tuple-element.80), channel_id=1, source_target_pairs={{8,0},{9,1},{10,2},{11,3},{12,4},{13,5},{14,6},{15,7},{0,8},{1,9},... | collective-permute-start | bytes 393224 | tf_op jit(solution)/shard_map/ppermute | solution.py:48
  36.8 14.6 %collective-permute-start.16 = (f32[64,512]{1,0:T(8,128)S(1)}, f32[64,512]{1,0:T(8,128)S(1)}, u32[]{:S(2)}, u32[]{:S(2)}) collective-permute-start(f32[64,512]{1,0:T(8,128)S(1)} %get-tuple-element.90.refs_4_), channel_id=1, source_target_pairs={{16,0},{0,16},{17,1},{1,17},{18,2},{2,18},{19,3},{3,19},{20,4},{4,... | collective-permute-start | bytes 393224 | tf_op jit(solution)/shard_map/ppermute | solution.py:48
  38.5 12.9 %collective-permute-start.17 = (f32[64,512]{1,0:T(8,128)S(1)}, f32[64,512]{1,0:T(8,128)S(1)}, u32[]{:S(2)}, u32[]{:S(2)}) collective-permute-start(f32[64,512]{1,0:T(8,128)S(1)} %get-tuple-element.94.refs_9_), channel_id=1, source_target_pairs={{16,0},{0,16},{17,1},{1,17},{18,2},{2,18},{19,3},{3,19},{20,4},{4,... | collective-permute-start | bytes 393224 | tf_op jit(solution)/shard_map/ppermute | solution.py:48
  40.3 3.7 %collective-permute-start.14 = (f32[64,256]{1,0:T(8,128)S(1)}, f32[64,256]{1,0:T(8,128)S(1)}, u32[]{:S(2)}, u32[]{:S(2)}) collective-permute-start(f32[64,256]{1,0:T(8,128)S(1)} %get-tuple-element.81.refs_16_), channel_id=1, source_target_pairs={{1,0},{2,1},{3,2},{4,3},{5,4},{6,5},{7,6},{8,7},{9,8},{10,9},{11,1... | collective-permute-start | bytes 196616 | tf_op jit(solution)/shard_map/ppermute | solution.py:48
  41.9 6.4 %collective-permute-start.13 = (f32[64,256]{1,0:T(8,128)S(1)}, f32[64,256]{1,0:T(8,128)S(1)}, u32[]{:S(2)}, u32[]{:S(2)}) collective-permute-start(f32[64,256]{1,0:T(8,128)S(1)} %get-tuple-element.82.refs_17_), channel_id=1, source_target_pairs={{15,0},{0,1},{1,2},{2,3},{3,4},{4,5},{5,6},{6,7},{7,8},{8,9},{9,10... | collective-permute-start | bytes 196616 | tf_op jit(solution)/shard_map/ppermute | solution.py:48
  44.0 10.0 %collective-permute-start.15 = (f32[64,512]{1,0:T(8,128)S(1)}, f32[64,512]{1,0:T(8,128)S(1)}, u32[]{:S(2)}, u32[]{:S(2)}) collective-permute-start(f32[64,512]{1,0:T(8,128)S(1)} %get-tuple-element.86.refs_9_), channel_id=1, source_target_pairs={{16,0},{0,16},{17,1},{1,17},{18,2},{2,18},{19,3},{3,19},{20,4},{4,... | collective-permute-start | bytes 393224 | tf_op jit(solution)/shard_map/ppermute | solution.py:48
  48.3 5.8 %collective-permute-start.11 = (f32[64,512]{1,0:T(8,128)S(1)}, f32[64,512]{1,0:T(8,128)S(1)}, u32[]{:S(2)}, u32[]{:S(2)}) collective-permute-start(f32[64,512]{1,0:T(8,128)S(1)} %get-tuple-element.77.refs_4_), channel_id=1, source_target_pairs={{16,0},{0,16},{17,1},{1,17},{18,2},{2,18},{19,3},{3,19},{20,4},{4,... | collective-permute-start | bytes 393224 | tf_op jit(solution)/shard_map/ppermute | solution.py:48
where the time goes:
time: 57 us; the launch traced here: 56.8 us
  starting transfers between devices  23.1 us (41%)
  Pallas kernels  20.6 us (36%)
  waiting for transfers between devices  7.04 us (12%)
  local copies, waits for them, and re-layouts  4.33 us (8%)
  between operations  1.71 us (3%)
    ppermute x18, starting transfers between devices, moved(): return lax.ppermute(block, axis, route)  23.1 us
    pallas_call x19, Pallas kernels, call(): pl.pallas_call(kernel, out_shape=out_shape, in_specs=in_specs, out_specs=...  20.6 us
    ppermute x18, waiting for transfers between devices, moved(): return lax.ppermute(block, axis, route)  7.04 us
    unnamed x8, local copies, waits for them, and re-layouts  4.33 us
  transfers between devices with their start and end apart: 18, of which 3 were waited for; matrix products, arithmetic and copies ran while one was open for 0% of the time, Pallas kernels for 30%

commit v1 on v0

--- a/solution.py
+++ b/solution.py
@@ -22,7 +22,7 @@
 CHUNKS = ((PX - 1, 0), (1, 2), (3, 4), (5, 6))
 EARLY = 2
 GROUP = 8
-FINISH = ((0, 1), (2, 3))
+FINISH = ((0, 1, 2, 3),)
 ROWS = 256
 LIMIT = 16 << 20
 
@@ -118,49 +118,72 @@
     return jax.ShapeDtypeStruct(shape, dtype)
 
 
-def prepare_kernel(tau, place, cov, xt, xe, gram, setup):
+def set_up(tau, place, setup):
     row = lax.broadcasted_iota(jnp.int32, setup.shape, 0)
     quantile = jnp.full(setup.shape, tau[0], jnp.int32).astype(F32) / QUANT
     pencil_y = jnp.full(setup.shape, place[0], jnp.int32)
     keep_prev = jnp.where(pencil_y > 0, 1.0, 0.0)
     keep_next = jnp.where(pencil_y < NPY - 1, 1.0, 0.0)
     setup[...] = jnp.where(row == 0, quantile, jnp.where(row == 1, keep_prev, keep_next))
-    high, low = halves(cov[...])
-    both = jnp.concatenate([high, low], 0)
-    xt[...] = both
-    turned = both.astype(F32).T.astype(BF16)
-    xe[...] = jnp.concatenate([turned, turned], 1)
-    summed = dot(both, turned)
-    summed = summed[:COVARS] + summed[COVARS:]
-    gram[...] = summed + pltpu.roll(summed, COVARS, 1)
-
-
-def prepare(tau, place, cov):
-    rows = cov.shape[1]
-    out = (sds(2 * COVARS, rows, dtype=BF16), sds(rows, 4 * COVARS, dtype=BF16), sds(COVARS, LANES), sds(8, LANES))
-    return call(prepare_kernel, out, [SMEM, SMEM, VMEM], (VMEM,) * 4, [], 1 << 24, (tau, place, cov))
-
-
-def first_kernel(layers, opening, *refs):
-    obs, xt, *gram, part = refs
+
+
+def opening_kernel(layers, tau, place, cov, far, part, xt, setup, cbuf, csem, ybuf, sems):
     width = len(layers) * LAYER
-    if opening:
-        part[:, width:] = gram[0][...]
+    fetch = pltpu.make_async_copy(cov, cbuf, csem)
+    fetch.start()
+    loads = copies(far, ybuf, sems, layers, True)
+    for row in loads:
+        start(row)
+    set_up(tau, place, setup)
+    fetch.wait()
+    high, low = halves(cbuf[...])
+    xt[...] = jnp.concatenate([high, low], 0)
+    gram = lax.dot_general(xt[...], xt[...], (((1,), (1,)), ((), ())), preferred_element_type=F32)
+    gram = gram[:COVARS] + gram[COVARS:]
+    part[:, width:] = gram + pltpu.roll(gram, COVARS, 1)
+    total = None
+    for block, row in enumerate(loads):
+        wait(row)
+        rows = slice(block * ROWS, (block + 1) * ROWS)
+        high, low = halves(ybuf[rows, :])
+        term = dot(xt[:, rows], high) + dot(xt[:, rows], low)
+        total = term if total is None else total + term
+    part[:, :width] = total[:COVARS] + total[COVARS:]
+
+
+def opening_stage(layers, tau, place, cov, far):
+    rows, width = far.shape[0], len(layers) * LAYER
+    out = (sds(COVARS, width + LANES), sds(2 * COVARS, rows, dtype=BF16), sds(8, LANES))
+    scratch = [
+        pltpu.VMEM(cov.shape, F32),
+        pltpu.SemaphoreType.DMA,
+        pltpu.VMEM((rows, width), F32),
+        pltpu.SemaphoreType.DMA((rows // ROWS, len(windows(layers)))),
+    ]
+    flops = 2 * rows * 2 * COVARS * 2 * width
+    kernel = functools.partial(opening_kernel, layers)
+    return call(kernel, out, [SMEM, SMEM, HBM, HBM], (VMEM,) * 3, scratch, flops, (tau, place, cov, far))
+
+
+def first_kernel(layers, turn, obs, xt, part, *xe):
     total = None
     for block in range(obs.shape[0] // ROWS):
         rows = slice(block * ROWS, (block + 1) * ROWS)
         high, low = halves(columns_of(obs, layers, rows))
         term = dot(xt[:, rows], high) + dot(xt[:, rows], low)
         total = term if total is None else total + term
-    part[:, :width] = total[:COVARS] + total[COVARS:]
-
-
-def first_stage(layers, args, opening):
-    rows, width = args[0].shape[0], len(layers) * LAYER
-    out = sds(COVARS, width + (LANES if opening else 0))
+    part[...] = total[:COVARS] + total[COVARS:]
+    if turn:
+        turned = xt[...].astype(F32).T.astype(BF16)
+        xe[0][...] = jnp.concatenate([turned, turned], 1)
+
+
+def first_stage(layers, obs, xt, turn):
+    rows, width = obs.shape[0], len(layers) * LAYER
+    out = (sds(COVARS, width),) + ((sds(rows, 4 * COVARS, dtype=BF16),) if turn else ())
     flops = 2 * rows * 2 * COVARS * 2 * width
-    kernel = functools.partial(first_kernel, layers, opening)
-    return call(kernel, out, [VMEM] * len(args), VMEM, [], flops, args)
+    kernel = functools.partial(first_kernel, layers, turn)
+    return call(kernel, out, [VMEM, VMEM], (VMEM,) * len(out), [], flops, (obs, xt))
 
 
 def packed_rows(chunks, lane):
@@ -475,12 +498,16 @@
     pencil_y = (lax.axis_index("vox") + NPY // 2) % pencils % NPY
     mask = voxel_mask.reshape(1, -1)
 
-    parts = []
-    xt, xe, gram, setup = prepare(tau_index, pencil_y.reshape(1), covariates.T)
+    parts, more = [], []
+    in_hbm = [pltpu.with_memory_space_constraint(a, pltpu.HBM) for a in (covariates.T, observed)]
     for number, layers in enumerate(CHUNKS):
-        args = [observed, xt] + ([] if number else [gram])
-        part = first_stage(layers, args, number == 0)
+        if number == 0:
+            part, xt, setup = opening_stage(layers, tau_index, pencil_y.reshape(1), *in_hbm)
+        else:
+            part, *turned = first_stage(layers, observed, xt, number == 1)
+            more += turned
         parts.append((part, others_sum(part, "sub")))
+    (xe,) = more
 
     eta, base, grad, states, fields = None, None, None, [None] * len(CHUNKS), []
     for stage in (1, 2):

time: 57 us -> 55.8 us (0.979)
  local copies, waits for them, and re-layouts: 4.33 us -> 0.01 us
  waiting for transfers between devices: 7.04 us -> 9.63 us
  Pallas kernels: 20.6 us -> 21.7 us
    unnamed x8 -> x4, local copies, waits for them, and re-layouts: 4.33 us -> 0.01 us
    ppermute x18, waiting for transfers between devices: 7.04 us -> 9.63 us  [moved(): return lax.ppermute(block, axis, route)]
    pallas_call x19 -> x17, Pallas kernels: 20.6 us -> 21.7 us  [call(): pl.pallas_call(kernel, out_shape=out_shape, in_specs=in_specs, out_specs=...]
  transfers between devices with their start and end apart: 18 -> 18, of which waited for: 3 -> 5; matrix products, arithmetic and copies ran while one was open for 0% -> 0% of each run, Pallas kernels for 30% -> 26%
where the time goes in v1:
time: 55.8 us; the launch traced here: 55.6 us
  starting transfers between devices  22.7 us (41%)
  Pallas kernels  21.7 us (39%)
  waiting for transfers between devices  9.63 us (17%)
  between operations  1.68 us (3%)
    ppermute x18, starting transfers between devices, moved(): return lax.ppermute(block, axis, route)  22.7 us
    pallas_call x17, Pallas kernels, call(): pl.pallas_call(kernel, out_shape=out_shape, in_specs=in_specs, out_specs=...  21.7 us
    ppermute x18, waiting for transfers between devices, moved(): return lax.ppermute(block, axis, route)  9.63 us
  transfers between devices with their start and end apart: 18, of which 5 were waited for; matrix products, arithmetic and copies ran while one was open for 0% of the time, Pallas kernels for 26%

profile of v1, /device:TPU:0, one launch (start us, length us, event | category | flops | bytes accessed | tf_op | source)
XLA Modules:
  0.0 55.6 jit_solution(12379316169790914402)
XLA Ops:
  1.3 0.0 copy-start
  1.3 3.0 %shard_map.59 = (f32[64,640]{1,0:T(8,128)S(1)}, bf16[128,1024]{1,0:T(8,128)(2,1)S(1)}, f32[8,128]{1,0:T(8,128)S(1)}) custom-call(s32[1]{0:T(128)S(6)} %copy.6.tau, s32[1]{0:T(128)} %bitcast.place, f32[64,1024]{1,0:T(8,128)} %bitcast.10, f32[1024,2048]{1,0:T(8,128)} %refs_4_.7), custom_call_target="tpu_custom_call" | custom-call | flops 268435456 | bytes 4194304 | tf_op jit(solution)/shard_map/pallas_call | solution.py:105
  4.3 3.0 %collective-permute-start = (f32[64,640]{1,0:T(8,128)S(1)}, f32[64,640]{1,0:T(8,128)S(1)}, u32[]{:S(2)}, u32[]{:S(2)}) collective-permute-start(f32[64,640]{1,0:T(8,128)S(1)} %get-tuple-element.51.refs_2_), channel_id=1, source_target_pairs={{16,0},{0,16},{17,1},{1,17},{18,2},{2,18},{19,3},{3,19},{20,4},{4,... | collective-permute-start | bytes 491528 | tf_op jit(solution)/shard_map/ppermute | solution.py:48
  7.3 0.0 copy-done
  7.3 0.5 shard_map.60
  7.8 1.1 %collective-permute-start.2 = (f32[64,512]{1,0:T(8,128)S(1)}, f32[64,512]{1,0:T(8,128)S(1)}, u32[]{:S(2)}, u32[]{:S(2)}) collective-permute-start(f32[64,512]{1,0:T(8,128)S(1)} %get-tuple-element.57.refs_2_), channel_id=1, source_target_pairs={{16,0},{0,16},{17,1},{1,17},{18,2},{2,18},{19,3},{3,19},{20,4},{4,... | collective-permute-start | bytes 393224 | tf_op jit(solution)/shard_map/ppermute | solution.py:48
  8.9 0.5 shard_map.63.refs_2_
  9.4 0.0 copy-start.1
  9.4 1.1 %collective-permute-start.3 = (f32[64,512]{1,0:T(8,128)S(1)}, f32[64,512]{1,0:T(8,128)S(1)}, u32[]{:S(2)}, u32[]{:S(2)}) collective-permute-start(f32[64,512]{1,0:T(8,128)S(1)} %shard_map.63.refs_2_), channel_id=1, source_target_pairs={{16,0},{0,16},{17,1},{1,17},{18,2},{2,18},{19,3},{3,19},{20,4},{4,... | collective-permute-start | bytes 393224 | tf_op jit(solution)/shard_map/ppermute | solution.py:48
  10.5 0.5 shard_map.64.refs_4_
  11.0 1.1 %collective-permute-start.4 = (f32[64,512]{1,0:T(8,128)S(1)}, f32[64,512]{1,0:T(8,128)S(1)}, u32[]{:S(2)}, u32[]{:S(2)}) collective-permute-start(f32[64,512]{1,0:T(8,128)S(1)} %shard_map.64.refs_4_), channel_id=1, source_target_pairs={{16,0},{0,16},{17,1},{1,17},{18,2},{2,18},{19,3},{3,19},{20,4},{4,... | collective-permute-start | bytes 393224 | tf_op jit(solution)/shard_map/ppermute | solution.py:48
  12.1 0.3 collective-permute-done.refs_3_
  12.4 0.0 copy-done.1
  12.4 1.1 %shard_map.61 = (f32[64,512]{1,0:T(8,128)S(1)}, f32[8,128]{1,0:T(8,128)S(1)}, f32[64,512]{1,0:T(8,128)S(1)}, f32[64,512]{1,0:T(8,128)S(1)}, f32[1024,512]{1,0:T(8,128)S(1)}) custom-call(f32[8,128]{1,0:T(8,128)S(1)} %get-tuple-element.50.refs_0_.edge_ref, s32[1,2048]{1,0:T(1,128)S(1)} %bitcast.3, f32[64,640]{1,0:T(8,128)S(1)} %get-tuple-element.51.refs_2_, ...), custom_call_target="tpu_custom_call" | custom-call | flops 536870912 | bytes 4194304 | tf_op jit(solution)/shard_map/pallas_call | solution.py:105
  13.5 3.2 %collective-permute-start.5 = (f32[64,512]{1,0:T(8,128)S(1)}, f32[64,512]{1,0:T(8,128)S(1)}, u32[]{:S(2)}, u32[]{:S(2)}) collective-permute-start(f32[64,512]{1,0:T(8,128)S(1)} %get-tuple-element.61), channel_id=1, source_target_pairs={{8,0},{9,1},{10,2},{11,3},{12,4},{13,5},{14,6},{15,7},{0,8},{1,9},... | collective-permute-start | bytes 393224 | tf_op jit(solution)/shard_map/ppermute | solution.py:48
  16.7 1.5 %collective-permute-start.1 = (f32[64,512]{1,0:T(8,128)S(1)}, f32[64,512]{1,0:T(8,128)S(1)}, u32[]{:S(2)}, u32[]{:S(2)}) collective-permute-start(f32[64,512]{1,0:T(8,128)S(1)} %get-tuple-element.55.refs_2_), channel_id=1, source_target_pairs={{16,0},{0,16},{17,1},{1,17},{18,2},{2,18},{19,3},{3,19},{20,4},{4,... | collective-permute-start | bytes 393224 | tf_op jit(solution)/shard_map/ppermute | solution.py:48
  18.2 0.0 collective-permute-done.2.refs_3_
  18.2 1.1 %shard_map.62 = (f32[64,512]{1,0:T(8,128)S(1)}, f32[64,512]{1,0:T(8,128)S(1)}, f32[1024,512]{1,0:T(8,128)S(1)}) custom-call(f32[8,128]{1,0:T(8,128)S(1)} %get-tuple-element.50.refs_0_.edge_ref, s32[1,2048]{1,0:T(1,128)S(1)} %bitcast.4, f32[64,512]{1,0:T(8,128)S(1)} %get-tuple-element.57.refs_2_, f32[64,512]{1,0:T(8,128)S(1)} %collective-permute-done.2.refs_3_, ...), custom_call_target="tpu_custom_call" | custom-call | flops 536870912 | bytes 4194304 | tf_op jit(solution)/shard_map/pallas_call | solution.py:105
  19.4 0.0 collective-permute-done.3.refs_3_
  19.4 1.5 %collective-permute-done.4.refs_5_ = f32[64,512]{1,0:T(8,128)S(1)} collective-permute-done((f32[64,512]{1,0:T(8,128)S(1)}, f32[64,512]{1,0:T(8,128)S(1)}, u32[]{:S(2)}, u32[]{:S(2)}) %collective-permute-start.4) | collective-permute-done | bytes 131104 | tf_op jit(solution)/shard_map/ppermute | solution.py:48
  20.8 0.2 shard_map.65
  21.0 2.6 %collective-permute-start.7 = (f32[64,256]{1,0:T(8,128)S(1)}, f32[64,256]{1,0:T(8,128)S(1)}, u32[]{:S(2)}, u32[]{:S(2)}) collective-permute-start(f32[64,256]{1,0:T(8,128)S(1)} %get-tuple-element.62.refs_6_), channel_id=1, source_target_pairs={{1,0},{2,1},{3,2},{4,3},{5,4},{6,5},{7,6},{8,7},{9,8},{10,9},{11,1... | collective-permute-start | bytes 196616 | tf_op jit(solution)/shard_map/ppermute | solution.py:48
  23.6 0.0 collective-permute-start.6
  23.6 1.5 %collective-permute-start.9 = (f32[64,512]{1,0:T(8,128)S(1)}, f32[64,512]{1,0:T(8,128)S(1)}, u32[]{:S(2)}, u32[]{:S(2)}) collective-permute-start(f32[64,512]{1,0:T(8,128)S(1)} %get-tuple-element.69.refs_2_), channel_id=1, source_target_pairs={{16,0},{0,16},{17,1},{1,17},{18,2},{2,18},{19,3},{3,19},{20,4},{4,... | collective-permute-start | bytes 393224 | tf_op jit(solution)/shard_map/ppermute | solution.py:48
  25.1 1.0 %shard_map.69 = (f32[64,512]{1,0:T(8,128)S(1)}, f32[1024,512]{1,0:T(8,128)S(1)}) custom-call(f32[8,128]{1,0:T(8,128)S(1)} %get-tuple-element.50.refs_0_.edge_ref, f32[64,512]{1,0:T(8,128)S(1)} %get-tuple-element.59.refs_2_.refs_1_.refs_4_, bf16[1024,256]{1,0:T(8,128)(2,1)S(1)} %get-tuple-element.53.refs_4_.refs_5_.refs_7_.refs_2_.refs_3_, ...), custom_call_target="tpu_custom_call" | custom-call | flops 536870912 | bytes 4194304 | tf_op jit(solution)/shard_map/pallas_call | solution.py:105
  26.2 1.0 %shard_map.70 = (f32[64,512]{1,0:T(8,128)S(1)}, f32[1024,512]{1,0:T(8,128)S(1)}) custom-call(f32[8,128]{1,0:T(8,128)S(1)} %get-tuple-element.50.refs_0_.edge_ref, f32[64,512]{1,0:T(8,128)S(1)} %get-tuple-element.60.refs_3_.refs_1_.refs_8_, bf16[1024,256]{1,0:T(8,128)(2,1)S(1)} %get-tuple-element.53.refs_4_.refs_5_.refs_7_.refs_2_.refs_3_, ...), custom_call_target="tpu_custom_call" | custom-call | flops 536870912 | bytes 4194304 | tf_op jit(solution)/shard_map/pallas_call | solution.py:105
  27.2 0.0 collective-permute-done.7.refs_9_
  27.2 0.6 %collective-permute-start.10 = (f32[64,512]{1,0:T(8,128)S(1)}, f32[64,512]{1,0:T(8,128)S(1)}, u32[]{:S(2)}, u32[]{:S(2)}) collective-permute-start(f32[64,512]{1,0:T(8,128)S(1)} %get-tuple-element.73.refs_2_), channel_id=1, source_target_pairs={{16,0},{0,16},{17,1},{1,17},{18,2},{2,18},{19,3},{3,19},{20,4},{4,... | collective-permute-start | bytes 393224 | tf_op jit(solution)/shard_map/ppermute | solution.py:48
  27.9 2.2 %collective-permute-done.6.refs_8_ = f32[64,256]{1,0:T(8,128)S(1)} collective-permute-done((f32[64,256]{1,0:T(8,128)S(1)}, f32[64,256]{1,0:T(8,128)S(1)}, u32[]{:S(2)}, u32[]{:S(2)}) %collective-permute-start.6) | collective-permute-done | bytes 65568 | tf_op jit(solution)/shard_map/ppermute | solution.py:48
  30.0 1.5 %collective-permute-start.11 = (f32[64,512]{1,0:T(8,128)S(1)}, f32[64,512]{1,0:T(8,128)S(1)}, u32[]{:S(2)}, u32[]{:S(2)}) collective-permute-start(f32[64,512]{1,0:T(8,128)S(1)} %get-tuple-element.75.refs_6_), channel_id=1, source_target_pairs={{16,0},{0,16},{17,1},{1,17},{18,2},{2,18},{19,3},{3,19},{20,4},{4,... | collective-permute-start | bytes 393224 | tf_op jit(solution)/shard_map/ppermute | solution.py:48
  31.5 0.0 collective-permute-done.5.refs_4_.refs_5_
  31.5 1.6 %shard_map.66 = (f32[64,512]{1,0:T(8,128)S(1)}, f32[64,512]{1,0:T(8,128)S(1)}, f32[64,512]{1,0:T(8,128)S(1)}, f32[64,512]{1,0:T(8,128)S(1)}) custom-call(f32[8,128]{1,0:T(8,128)S(1)} %get-tuple-element.50.refs_0_.edge_ref, f32[64,512]{1,0:T(8,128)S(1)} %get-tuple-element.56.refs_6_.refs_0_.refs_5_, f32[64,512]{1,0:T(8,128)S(1)} %get-tuple-element.58.refs_7_.refs_1_.refs_5_, ...), custom_call_target="tpu_custom_call" | custom-call | flops 503316480 | bytes 4194304 | tf_op jit(solution)/shard_map/pallas_call | solution.py:105
  33.2 0.0 collective-permute-done.9.refs_3_
  33.2 1.1 %shard_map.68 = (f32[64,512]{1,0:T(8,128)S(1)}, f32[64,512]{1,0:T(8,128)S(1)}, f32[64,512]{1,0:T(8,128)S(1)}, f32[1024,512]{1,0:T(8,128)S(1)}) custom-call(f32[8,128]{1,0:T(8,128)S(1)} %get-tuple-element.50.refs_0_.edge_ref, s32[1,2048]{1,0:T(1,128)S(1)} %bitcast.6, f32[64,512]{1,0:T(8,128)S(1)} %get-tuple-element.69.refs_2_, ...), custom_call_target="tpu_custom_call" | custom-call | flops 536870912 | bytes 4194304 | tf_op jit(solution)/shard_map/pallas_call | solution.py:105
  34.3 0.6 %collective-permute-start.15 = (f32[64,512]{1,0:T(8,128)S(1)}, f32[64,512]{1,0:T(8,128)S(1)}, u32[]{:S(2)}, u32[]{:S(2)}) collective-permute-start(f32[64,512]{1,0:T(8,128)S(1)} %get-tuple-element.84.refs_9_), channel_id=1, source_target_pairs={{16,0},{0,16},{17,1},{1,17},{18,2},{2,18},{19,3},{3,19},{20,4},{4,... | collective-permute-start | bytes 393224 | tf_op jit(solution)/shard_map/ppermute | solution.py:48
  34.9 0.0 collective-permute-done.1.refs_3_
  34.9 1.1 %shard_map.67 = (f32[64,512]{1,0:T(8,128)S(1)}, f32[64,512]{1,0:T(8,128)S(1)}, f32[64,512]{1,0:T(8,128)S(1)}, f32[64,512]{1,0:T(8,128)S(1)}, f32[1024,512]{1,0:T(8,128)S(1)}) custom-call(f32[8,128]{1,0:T(8,128)S(1)} %get-tuple-element.50.refs_0_.edge_ref, s32[1,2048]{1,0:T(1,128)S(1)} %bitcast.7, f32[64,512]{1,0:T(8,128)S(1)} %get-tuple-element.55.refs_2_, ...), custom_call_target="tpu_custom_call" | custom-call | flops 536870912 | bytes 4194304 | tf_op jit(solution)/shard_map/pallas_call | solution.py:105
  36.1 0.1 collective-permute-start.12
  36.2 1.6 %collective-permute-start.8 = (f32[64,512]{1,0:T(8,128)S(1)}, f32[64,512]{1,0:T(8,128)S(1)}, u32[]{:S(2)}, u32[]{:S(2)}) collective-permute-start(f32[64,512]{1,0:T(8,128)S(1)} %get-tuple-element.66.refs_4_), channel_id=1, source_target_pairs={{16,0},{0,16},{17,1},{1,17},{18,2},{2,18},{19,3},{3,19},{20,4},{4,... | collective-permute-start | bytes 393224 | tf_op jit(solution)/shard_map/ppermute | solution.py:48
  37.7 0.0 collective-permute-done.10.refs_3_
  37.7 0.0 collective-permute-done.11.refs_7_
  37.7 0.2 shard_map.71
  38.0 2.1 %collective-permute-start.14 = (f32[64,256]{1,0:T(8,128)S(1)}, f32[64,256]{1,0:T(8,128)S(1)}, u32[]{:S(2)}, u32[]{:S(2)}) collective-permute-start(f32[64,256]{1,0:T(8,128)S(1)} %get-tuple-element.80.refs_16_), channel_id=1, source_target_pairs={{1,0},{2,1},{3,2},{4,3},{5,4},{6,5},{7,6},{8,7},{9,8},{10,9},{11,1... | collective-permute-start | bytes 196616 | tf_op jit(solution)/shard_map/ppermute | solution.py:48
  40.1 0.0 collective-permute-start.13
  40.1 1.1 %shard_map.74 = (f32[64,512]{1,0:T(8,128)S(1)}, f32[1024,512]{1,0:T(8,128)S(1)}) custom-call(f32[8,128]{1,0:T(8,128)S(1)} %get-tuple-element.50.refs_0_.edge_ref, f32[64,512]{1,0:T(8,128)S(1)} %get-tuple-element.78.refs_13_.refs_1_, bf16[1024,256]{1,0:T(8,128)(2,1)S(1)} %get-tuple-element.53.refs_4_.refs_5_.refs_7_.refs_2_.refs_3_, ...), custom_call_target="tpu_custom_call" | custom-call | flops 536870912 | bytes 4194304 | tf_op jit(solution)/shard_map/pallas_call | solution.py:105
  41.2 1.1 %shard_map.73 = (f32[64,512]{1,0:T(8,128)S(1)}, f32[1024,512]{1,0:T(8,128)S(1)}) custom-call(f32[8,128]{1,0:T(8,128)S(1)} %get-tuple-element.50.refs_0_.edge_ref, f32[64,512]{1,0:T(8,128)S(1)} %get-tuple-element.77.refs_12_.refs_1_, bf16[1024,256]{1,0:T(8,128)(2,1)S(1)} %get-tuple-element.53.refs_4_.refs_5_.refs_7_.refs_2_.refs_3_, ...), custom_call_target="tpu_custom_call" | custom-call | flops 536870912 | bytes 4194304 | tf_op jit(solution)/shard_map/pallas_call | solution.py:105
  42.2 0.0 collective-permute-done.14.refs_19_
  42.2 0.6 %collective-permute-start.17 = (f32[64,512]{1,0:T(8,128)S(1)}, f32[64,512]{1,0:T(8,128)S(1)}, u32[]{:S(2)}, u32[]{:S(2)}) collective-permute-start(f32[64,512]{1,0:T(8,128)S(1)} %get-tuple-element.94.refs_19_), channel_id=1, source_target_pairs={{16,0},{0,16},{17,1},{1,17},{18,2},{2,18},{19,3},{3,19},{20,4},{4,... | collective-permute-start | bytes 393224 | tf_op jit(solution)/shard_map/ppermute | solution.py:48
  42.8 3.6 %collective-permute-done.13.refs_18_ = f32[64,256]{1,0:T(8,128)S(1)} collective-permute-done((f32[64,256]{1,0:T(8,128)S(1)}, f32[64,256]{1,0:T(8,128)S(1)}, u32[]{:S(2)}, u32[]{:S(2)}) %collective-permute-start.13) | collective-permute-done | bytes 65568 | tf_op jit(solution)/shard_map/ppermute | solution.py:48
  46.5 0.5 collective-permute-start.16
  47.0 0.0 collective-permute-done.12.refs_14_.refs_15_
  47.0 2.4 %shard_map.72 = (f32[64,512]{1,0:T(8,128)S(1)}, f32[64,512]{1,0:T(8,128)S(1)}, f32[64,512]{1,0:T(8,128)S(1)}, f32[64,512]{1,0:T(8,128)S(1)}) custom-call(f32[8,128]{1,0:T(8,128)S(1)} %get-tuple-element.50.refs_0_.edge_ref, f32[64,512]{1,0:T(8,128)S(1)} %get-tuple-element.56.refs_6_.refs_0_.refs_5_, f32[64,512]{1,0:T(8,128)S(1)} %get-tuple-element.58.refs_7_.refs_1_.refs_5_, ...), custom_call_target="tpu_custom_call" | custom-call | flops 1006632960 | bytes 4194304 | tf_op jit(solution)/shard_map/pallas_call | solution.py:105
  49.4 0.0 collective-permute-done.15.refs_10_
  49.4 0.0 collective-permute-done.8.refs_5_
  49.4 0.0 collective-permute-done.17.refs_20_
  49.4 2.0 %collective-permute-done.16.refs_15_ = f32[64,512]{1,0:T(8,128)S(1)} collective-permute-done((f32[64,512]{1,0:T(8,128)S(1)}, f32[64,512]{1,0:T(8,128)S(1)}, u32[]{:S(2)}, u32[]{:S(2)}) %collective-permute-start.16) | collective-permute-done | bytes 131104 | tf_op jit(solution)/shard_map/ppermute | solution.py:48
  51.4 4.0 %shard_map.75 = (f32[64,2048]{1,0:T(8,128)}, f32[1024,2048]{1,0:T(8,128)}) custom-call(f32[8,128]{1,0:T(8,128)S(1)} %get-tuple-element.50.refs_0_.edge_ref, s32[1,2048]{1,0:T(1,128)S(1)} %bitcast.9, f32[8,128]{1,0:T(8,128)S(1)} %get-tuple-element.54.refs_4_.refs_1_.refs_2_, bf16[1024,256]{1,0:T(8,128)(2,1)S(1)} %get-tuple-element.53.refs_4_.refs_5_.refs_7_.refs_2_.refs_3_, ...), custom_call_target="tpu_custom_call" | custom-call | flops 2147483648 | bytes 4194304 | tf_op jit(solution)/shard_map/pallas_call | solution.py:105
Async XLA Ops:
  1.3 6.0 %copy-start = (f32[1024,2048]{1,0:T(8,128)S(1)}, f32[1024,2048]{1,0:T(8,128)}, u32[]{:S(2)}) copy-start(f32[1024,2048]{1,0:T(8,128)} %refs_4_.7) | copy-start | bytes 25165828
  4.3 8.1 %collective-permute-start = (f32[64,640]{1,0:T(8,128)S(1)}, f32[64,640]{1,0:T(8,128)S(1)}, u32[]{:S(2)}, u32[]{:S(2)}) collective-permute-start(f32[64,640]{1,0:T(8,128)S(1)} %get-tuple-element.51.refs_2_), channel_id=1, source_target_pairs={{16,0},{0,16},{17,1},{1,17},{18,2},{2,18},{19,3},{3,19},{20,4},{4,... | collective-permute-start | bytes 491528 | tf_op jit(solution)/shard_map/ppermute | solution.py:48
  7.8 10.4 %collective-permute-start.2 = (f32[64,512]{1,0:T(8,128)S(1)}, f32[64,512]{1,0:T(8,128)S(1)}, u32[]{:S(2)}, u32[]{:S(2)}) collective-permute-start(f32[64,512]{1,0:T(8,128)S(1)} %get-tuple-element.57.refs_2_), channel_id=1, source_target_pairs={{16,0},{0,16},{17,1},{1,17},{18,2},{2,18},{19,3},{3,19},{20,4},{4,... | collective-permute-start | bytes 393224 | tf_op jit(solution)/shard_map/ppermute | solution.py:48
  9.4 3.0 %copy-start.1 = (s32[2048]{0:T(1024)S(1)}, s32[2048]{0:T(1024)}, u32[]{:S(2)}) copy-start(s32[2048]{0:T(1024)} %param.6) | copy-start | bytes 24580
  9.4 9.9 %collective-permute-start.3 = (f32[64,512]{1,0:T(8,128)S(1)}, f32[64,512]{1,0:T(8,128)S(1)}, u32[]{:S(2)}, u32[]{:S(2)}) collective-permute-start(f32[64,512]{1,0:T(8,128)S(1)} %shard_map.63.refs_2_), channel_id=1, source_target_pairs={{16,0},{0,16},{17,1},{1,17},{18,2},{2,18},{19,3},{3,19},{20,4},{4,... | collective-permute-start | bytes 393224 | tf_op jit(solution)/shard_map/ppermute | solution.py:48
  11.0 9.8 %collective-permute-start.4 = (f32[64,512]{1,0:T(8,128)S(1)}, f32[64,512]{1,0:T(8,128)S(1)}, u32[]{:S(2)}, u32[]{:S(2)}) collective-permute-start(f32[64,512]{1,0:T(8,128)S(1)} %shard_map.64.refs_4_), channel_id=1, source_target_pairs={{16,0},{0,16},{17,1},{1,17},{18,2},{2,18},{19,3},{3,19},{20,4},{4,... | collective-permute-start | bytes 393224 | tf_op jit(solution)/shard_map/ppermute | solution.py:48
  13.5 18.0 %collective-permute-start.5 = (f32[64,512]{1,0:T(8,128)S(1)}, f32[64,512]{1,0:T(8,128)S(1)}, u32[]{:S(2)}, u32[]{:S(2)}) collective-permute-start(f32[64,512]{1,0:T(8,128)S(1)} %get-tuple-element.61), channel_id=1, source_target_pairs={{8,0},{9,1},{10,2},{11,3},{12,4},{13,5},{14,6},{15,7},{0,8},{1,9},... | collective-permute-start | bytes 393224 | tf_op jit(solution)/shard_map/ppermute | solution.py:48
  16.7 18.2 %collective-permute-start.1 = (f32[64,512]{1,0:T(8,128)S(1)}, f32[64,512]{1,0:T(8,128)S(1)}, u32[]{:S(2)}, u32[]{:S(2)}) collective-permute-start(f32[64,512]{1,0:T(8,128)S(1)} %get-tuple-element.55.refs_2_), channel_id=1, source_target_pairs={{16,0},{0,16},{17,1},{1,17},{18,2},{2,18},{19,3},{3,19},{20,4},{4,... | collective-permute-start | bytes 393224 | tf_op jit(solution)/shard_map/ppermute | solution.py:48
  21.0 6.2 %collective-permute-start.7 = (f32[64,256]{1,0:T(8,128)S(1)}, f32[64,256]{1,0:T(8,128)S(1)}, u32[]{:S(2)}, u32[]{:S(2)}) collective-permute-start(f32[64,256]{1,0:T(8,128)S(1)} %get-tuple-element.62.refs_6_), channel_id=1, source_target_pairs={{1,0},{2,1},{3,2},{4,3},{5,4},{6,5},{7,6},{8,7},{9,8},{10,9},{11,1... | collective-permute-start | bytes 196616 | tf_op jit(solution)/shard_map/ppermute | solution.py:48
  23.6 6.4 %collective-permute-start.6 = (f32[64,256]{1,0:T(8,128)S(1)}, f32[64,256]{1,0:T(8,128)S(1)}, u32[]{:S(2)}, u32[]{:S(2)}) collective-permute-start(f32[64,256]{1,0:T(8,128)S(1)} %get-tuple-element.63.refs_7_), channel_id=1, source_target_pairs={{15,0},{0,1},{1,2},{2,3},{3,4},{4,5},{5,6},{6,7},{7,8},{8,9},{9,10... | collective-permute-start | bytes 196616 | tf_op jit(solution)/shard_map/ppermute | solution.py:48
  23.6 9.5 %collective-permute-start.9 = (f32[64,512]{1,0:T(8,128)S(1)}, f32[64,512]{1,0:T(8,128)S(1)}, u32[]{:S(2)}, u32[]{:S(2)}) collective-permute-start(f32[64,512]{1,0:T(8,128)S(1)} %get-tuple-element.69.refs_2_), channel_id=1, source_target_pairs={{16,0},{0,16},{17,1},{1,17},{18,2},{2,18},{19,3},{3,19},{20,4},{4,... | collective-permute-start | bytes 393224 | tf_op jit(solution)/shard_map/ppermute | solution.py:48
  27.2 10.5 %collective-permute-start.10 = (f32[64,512]{1,0:T(8,128)S(1)}, f32[64,512]{1,0:T(8,128)S(1)}, u32[]{:S(2)}, u32[]{:S(2)}) collective-permute-start(f32[64,512]{1,0:T(8,128)S(1)} %get-tuple-element.73.refs_2_), channel_id=1, source_target_pairs={{16,0},{0,16},{17,1},{1,17},{18,2},{2,18},{19,3},{3,19},{20,4},{4,... | collective-permute-start | bytes 393224 | tf_op jit(solution)/shard_map/ppermute | solution.py:48
  30.0 7.7 %collective-permute-start.11 = (f32[64,512]{1,0:T(8,128)S(1)}, f32[64,512]{1,0:T(8,128)S(1)}, u32[]{:S(2)}, u32[]{:S(2)}) collective-permute-start(f32[64,512]{1,0:T(8,128)S(1)} %get-tuple-element.75.refs_6_), channel_id=1, source_target_pairs={{16,0},{0,16},{17,1},{1,17},{18,2},{2,18},{19,3},{3,19},{20,4},{4,... | collective-permute-start | bytes 393224 | tf_op jit(solution)/shard_map/ppermute | solution.py:48
  34.3 15.1 %collective-permute-start.15 = (f32[64,512]{1,0:T(8,128)S(1)}, f32[64,512]{1,0:T(8,128)S(1)}, u32[]{:S(2)}, u32[]{:S(2)}) collective-permute-start(f32[64,512]{1,0:T(8,128)S(1)} %get-tuple-element.84.refs_9_), channel_id=1, source_target_pairs={{16,0},{0,16},{17,1},{1,17},{18,2},{2,18},{19,3},{3,19},{20,4},{4,... | collective-permute-start | bytes 393224 | tf_op jit(solution)/shard_map/ppermute | solution.py:48
  36.1 10.9 %collective-permute-start.12 = (f32[64,512]{1,0:T(8,128)S(1)}, f32[64,512]{1,0:T(8,128)S(1)}, u32[]{:S(2)}, u32[]{:S(2)}) collective-permute-start(f32[64,512]{1,0:T(8,128)S(1)} %get-tuple-element.79), channel_id=1, source_target_pairs={{8,0},{9,1},{10,2},{11,3},{12,4},{13,5},{14,6},{15,7},{0,8},{1,9},... | collective-permute-start | bytes 393224 | tf_op jit(solution)/shard_map/ppermute | solution.py:48
  36.2 13.3 %collective-permute-start.8 = (f32[64,512]{1,0:T(8,128)S(1)}, f32[64,512]{1,0:T(8,128)S(1)}, u32[]{:S(2)}, u32[]{:S(2)}) collective-permute-start(f32[64,512]{1,0:T(8,128)S(1)} %get-tuple-element.66.refs_4_), channel_id=1, source_target_pairs={{16,0},{0,16},{17,1},{1,17},{18,2},{2,18},{19,3},{3,19},{20,4},{4,... | collective-permute-start | bytes 393224 | tf_op jit(solution)/shard_map/ppermute | solution.py:48
  38.0 4.2 %collective-permute-start.14 = (f32[64,256]{1,0:T(8,128)S(1)}, f32[64,256]{1,0:T(8,128)S(1)}, u32[]{:S(2)}, u32[]{:S(2)}) collective-permute-start(f32[64,256]{1,0:T(8,128)S(1)} %get-tuple-element.80.refs_16_), channel_id=1, source_target_pairs={{1,0},{2,1},{3,2},{4,3},{5,4},{6,5},{7,6},{8,7},{9,8},{10,9},{11,1... | collective-permute-start | bytes 196616 | tf_op jit(solution)/shard_map/ppermute | solution.py:48
  40.1 6.4 %collective-permute-start.13 = (f32[64,256]{1,0:T(8,128)S(1)}, f32[64,256]{1,0:T(8,128)S(1)}, u32[]{:S(2)}, u32[]{:S(2)}) collective-permute-start(f32[64,256]{1,0:T(8,128)S(1)} %get-tuple-element.81.refs_17_), channel_id=1, source_target_pairs={{15,0},{0,1},{1,2},{2,3},{3,4},{4,5},{5,6},{6,7},{7,8},{8,9},{9,10... | collective-permute-start | bytes 196616 | tf_op jit(solution)/shard_map/ppermute | solution.py:48
  42.2 7.2 %collective-permute-start.17 = (f32[64,512]{1,0:T(8,128)S(1)}, f32[64,512]{1,0:T(8,128)S(1)}, u32[]{:S(2)}, u32[]{:S(2)}) collective-permute-start(f32[64,512]{1,0:T(8,128)S(1)} %get-tuple-element.94.refs_19_), channel_id=1, source_target_pairs={{16,0},{0,16},{17,1},{1,17},{18,2},{2,18},{19,3},{3,19},{20,4},{4,... | collective-permute-start | bytes 393224 | tf_op jit(solution)/shard_map/ppermute | solution.py:48
  46.5 5.0 %collective-permute-start.16 = (f32[64,512]{1,0:T(8,128)S(1)}, f32[64,512]{1,0:T(8,128)S(1)}, u32[]{:S(2)}, u32[]{:S(2)}) collective-permute-start(f32[64,512]{1,0:T(8,128)S(1)} %get-tuple-element.89.refs_14_), channel_id=1, source_target_pairs={{16,0},{0,16},{17,1},{1,17},{18,2},{2,18},{19,3},{3,19},{20,4},{4,... | collective-permute-start | bytes 393224 | tf_op jit(solution)/shard_map/ppermute | solution.py:48
